TPU v7x, 32 devices: a whole 2x2x4 slice. The times are simulated.
32 devices in a mesh: lat: 8 (over z, core), rad: 4 (over y, x).
Axes of the slice: x: 2, y: 2, z: 4, core: 2. Of those that a mesh axis runs over, the one named last changes fastest.
Arguments:
- residual: float32 [3, 32, 64, 256], P(None, 'rad', 'lat'), may hold values from -30 to 30
- prev_basis: float32 [4, 3, 32, 64, 256], P(None, None, 'rad', 'lat'), may hold values from -30 to 30
- layer_ids: int32 [16, 32, 128], P('rad', 'lat'), may hold values from 0 to 7
- viscosity: float32 [8], replicated, may hold values from 0.1 to 1
- shifts: float32 [4], replicated, may hold values from 0.3 to 2
Outputs:
- new_basis: float32 [4, 3, 32, 64, 256], P(None, None, 'rad', 'lat')
- gram_matrix: float32 [9, 9], replicated
All inputs are finite; a program needn't handle non-finite values.
Results may differ from a plain program's by a relative error of at most 0.00019.
Values sent between devices are 32-bit elements; how exact they have to be, the bound alone decides.
A program may use at most 128 MiB of HBM per device.

v0:
```python
import functools

import jax
import jax.numpy as jnp
from jax import lax
from jax.experimental import pallas as pl
from jax.experimental.pallas import tpu as pltpu
from jax.sharding import PartitionSpec as P

MESH = pl.DeviceIdType.MESH
F32 = jnp.float32

mass = (1.0 / 36, 1.0 / 12, 1.0 / 45)
stiff = (0.0, 1.0, 4.0 / 3)

DIRS = ((-1, -1), (-1, 0), (-1, 1), (0, -1), (0, 1), (1, -1), (1, 0), (1, 1))
SLOT = {d: i for i, d in enumerate(DIRS)}
R_DIRS = {(-1, 0): 0, (1, 0): 1}
X_DIRS = {(0, -1): 0, (0, 1): 1}
C_DIRS = {(-1, -1): 0, (-1, 1): 1, (1, -1): 2, (1, 1): 3}
FIRST = ((-1, 0), (0, -1), (-1, -1))
LAST = ((1, 0), (0, 1), (1, 1))


def weight(a, b, c):
    return (
        stiff[a] * mass[b] * mass[c] + mass[a] * stiff[b] * mass[c] + mass[a] * mass[b] * stiff[c]
    )


def forward(u0, u1, u2):
    total = u0 + u2
    twice = u1 + u1
    return total + (twice + twice), u0 - u2, total - twice


def backward(m0, m1, m2):
    both = m0 + m2
    half = m0 + m0 - m2
    return both + m1, half + half, both - m1


def kernel(
    n_lat,
    n_rad,
    n_steps,
    n_prev,
    comps,
    res_ref,
    prev_ref,
    ids_ref,
    visc_ref,
    shift_ref,
    out_ref,
    gram_ref,
    stage,
    back,
    work,
    vec,
    ghost_r,
    ghost_x,
    ghost_c,
    scaled,
    send_r,
    send_x,
    send_c,
    recv_r,
    recv_x,
    recv_c,
    gram_send,
    gram_recv,
    in_sem,
    out_sem,
    send_sem,
    recv_sem,
    gram_sems,
):
    n_dev = n_lat * n_rad
    lat = lax.axis_index("lat")
    rad = lax.axis_index("rad")
    me = lat * n_rad + rad
    rows = res_ref.shape[0]
    half_y = res_ref.shape[1] // 2
    n_vec = n_prev + n_steps + 1

    res_copy = pltpu.make_async_copy(res_ref, stage.at[n_prev], in_sem.at[0])
    res_copy.start()
    prev_copy = pltpu.make_async_copy(prev_ref, stage.at[pl.ds(0, n_prev)], in_sem.at[1])
    prev_copy.start()

    recv_r[...] = jnp.zeros_like(recv_r)
    recv_x[...] = jnp.zeros_like(recv_x)
    recv_c[...] = jnp.zeros_like(recv_c)

    barrier = pltpu.get_barrier_semaphore()

    def other(d):
        t = lax.rem(me + d, n_dev)
        return {"lat": t // n_rad, "rad": lax.rem(t, n_rad)}

    def greet(d, carry):
        pl.semaphore_signal(barrier, inc=1, device_id=other(d), device_id_type=MESH)
        return carry

    lax.fori_loop(1, n_dev, greet, 0)

    sub = lax.broadcasted_iota(jnp.int32, (8, half_y), 0)
    lane = lax.broadcasted_iota(jnp.int32, (8, half_y), 1)
    upper = sub >= 4
    ex = lax.rem(sub, 4)
    first_x = ex == 0
    last_x = ex == 3
    corner0 = sub == 0
    corner3 = sub == 3
    corner4 = sub == 4
    corner7 = sub == 7
    has_up = rad < n_rad - 1
    has_right = lat < n_lat - 1
    up_f = jnp.where(has_up, 1.0, 0.0).astype(F32)
    right_f = jnp.where(has_right, 1.0, 0.0).astype(F32)
    both_f = up_f * right_f

    def roll_s(v, k):
        return pltpu.roll(v, k % 8, 0)

    def keep(mask, v):
        return jnp.where(mask, v, 0.0)

    src = lax.broadcasted_iota(jnp.int32, (2 * half_y, 2 * half_y), 0)
    dst = lax.broadcasted_iota(jnp.int32, (2 * half_y, 2 * half_y), 1)
    split_perm = jnp.where(
        src == jnp.where(dst < half_y, 2 * dst, 2 * (dst - half_y) + 1), 1.0, 0.0
    ).astype(F32)
    join_perm = jnp.where(
        dst == jnp.where(src < half_y, 2 * src, 2 * (src - half_y) + 1), 1.0, 0.0
    ).astype(F32)

    def exact_dot(a, b):
        return jnp.dot(a, b, precision=lax.Precision.HIGHEST, preferred_element_type=F32)

    def split_columns(i):
        z = exact_dot(stage[i], split_perm)
        work[i, 0] = z[:, :half_y]
        work[i, 1] = z[:, half_y:]

    def native(c, ro, p, h):
        return pl.ds(c * 64 + (4 * h + ro) * 8 + p, 4, stride=2)

    kinds = {}
    for a in range(3):
        for b in range(3):
            for c in range(3):
                key = tuple(sorted((a, b, c)))
                if key != (0, 0, 0) and key not in kinds:
                    kinds[key] = len(kinds)
    for e in range(2):
        ids = jnp.concatenate([ids_ref[e], ids_ref[2 + e]], 0)
        eta = jnp.zeros((8, half_y), F32)
        for layer in range(visc_ref.shape[0]):
            eta = eta + jnp.where(ids == layer, visc_ref[layer], 0.0)
        for key, i in kinds.items():
            scaled[e, i] = eta * weight(*key)

    def copy_of(step, d):
        if d in R_DIRS:
            a, b = send_r.at[step, R_DIRS[d]], recv_r.at[step, R_DIRS[d]]
        elif d in X_DIRS:
            a, b = send_x.at[step, X_DIRS[d]], recv_x.at[step, X_DIRS[d]]
        else:
            a, b = send_c.at[step, C_DIRS[d]], recv_c.at[step, C_DIRS[d]]
        return pltpu.make_async_remote_copy(
            src_ref=a,
            dst_ref=b,
            send_sem=send_sem.at[step, SLOT[d]],
            recv_sem=recv_sem.at[step, SLOT[d]],
            device_id={"lat": lat + d[1], "rad": rad + d[0]},
            device_id_type=MESH,
        )

    def inside(dr, dx):
        ok = None
        for pos, step, count in ((rad, dr, n_rad), (lat, dx, n_lat)):
            if step:
                one = (pos > 0) if step < 0 else (pos < count - 1)
                ok = one if ok is None else jnp.logical_and(ok, one)
        return ok

    order = ((-1, -1), (1, 1), (-1, 1), (1, -1), (1, 0), (-1, 0), (0, 1), (0, -1))

    def dirs_of(step):
        wanted = FIRST if step == 0 else (LAST if step == n_steps else DIRS)
        return [d for d in order if d in wanted]

    def start_round(step):
        for d in dirs_of(step):

            @pl.when(inside(*d))
            def _(d=d):
                copy_of(step, d).start()

    def finish_round(step):
        for d in dirs_of(step):

            @pl.when(inside(-d[0], -d[1]))
            def _(d=d):
                copy_of(step, d).wait_recv()

    def pack_x(vals, at):
        out = None
        for ro in range(4):
            moved = roll_s(vals[ro], ro - at)
            out = moved if out is None else jnp.where(ex == ro, moved, out)
        return out

    def apply(k, c):
        s = shift_ref[k]
        cur = k % 2
        new = 1 - cur
        u = {}
        gx = {}
        for q in range(2):
            for ro in range(4):
                gx[ro, q] = ghost_x[cur, c, ro, q]
                for p in range(2):
                    u[ro, p, q] = vec[cur, c, ro, p, q]
            gx[4, q] = jnp.where(upper, ghost_c[cur, c, q], roll_s(gx[0, q], 4))
            for p in range(2):
                u[4, p, q] = jnp.where(upper, ghost_r[cur, c, p, q], roll_s(u[0, p, q], 4))
            for ro in range(5):
                u[ro, 2, q] = jnp.where(last_x, gx[ro, q], roll_s(u[ro, 0, q], -1))
        res = {}
        for e in range(2):
            t = {}
            for p in range(3):
                for q in range(2):
                    t[0, p, q], t[1, p, q], t[2, p, q] = forward(
                        u[2 * e, p, q], u[2 * e + 1, p, q], u[2 * e + 2, p, q]
                    )
            w = {}
            for a in range(3):
                x = {}
                for q in range(2):
                    x[0, q], x[1, q], x[2, q] = forward(t[a, 0, q], t[a, 1, q], t[a, 2, q])
                for b in range(3):
                    nxt = keep(lane != half_y - 1, pltpu.roll(x[b, 0], half_y - 1, 1))
                    m = list(forward(x[b, 0], x[b, 1], nxt))
                    for j in range(3):
                        key = tuple(sorted((a, b, j)))
                        if key in kinds:
                            m[j] = m[j] * scaled[e, kinds[key]]
                        else:
                            m[j] = None
                    if m[0] is None:
                        r0 = m[1] + m[2]
                        r1 = -(m[2] + m[2])
                        r2 = m[2] - m[1]
                    else:
                        r0, r1, r2 = backward(*m)
                    x[b, 0] = r0 + keep(lane != 0, pltpu.roll(r2, 1, 1))
                    x[b, 1] = r1
                for q in range(2):
                    w[a, 0, q], w[a, 1, q], w[a, 2, q] = backward(x[0, q], x[1, q], x[2, q])
            for p in range(3):
                for q in range(2):
                    r = backward(w[0, p, q], w[1, p, q], w[2, p, q])
                    for i in range(3):
                        key = (2 * e + i, p, q)
                        res[key] = res[key] + r[i] if key in res else r[i]
        px = {}
        for q in range(2):
            for ro in range(5):
                edge = res[ro, 2, q]
                px[ro, q] = edge
                res[ro, 0, q] = res[ro, 0, q] + keep(ex != 0, roll_s(edge, 1))
            for p in range(2):
                res[0, p, q] = res[0, p, q] + keep(upper, roll_s(res[4, p, q], 4))
            px[0, q] = px[0, q] + keep(upper, roll_s(px[4, q], 4))
        step = k + 1
        last = step == n_steps
        for q in range(2):
            i = 2 * c + q
            row = slice(i, i + 1)
            send_r[step, 1, i] = jnp.where(upper, res[4, 1, q], roll_s(res[4, 0, q], 4))
            send_r[step, 1, 2 * comps, row] = px[4, q][7:8]
            send_x[step, 1, i] = pack_x([px[ro, q] for ro in range(4)], 3)
            send_x[step, 1, 2 * comps, row] = px[4, q][7:8]
            send_c[step, 3, row] = px[4, q][7:8]
            if not last:
                send_r[step, 0, i] = jnp.where(upper, roll_s(res[0, 1, q], 4), res[0, 0, q])
                send_r[step, 0, 2 * comps, row] = px[0, q][3:4]
                send_x[step, 0, i] = pack_x([res[ro, 0, q] for ro in range(4)], 0)
                send_x[step, 0, 2 * comps, row] = res[4, 0, q][4:5]
                send_c[step, 0, row] = res[0, 0, q][0:1]
                send_c[step, 1, row] = px[0, q][3:4]
                send_c[step, 2, row] = res[4, 0, q][4:5]
            for ro in range(4):
                for p in range(2):
                    vec[new, c, ro, p, q] = res[ro, p, q] - s * u[ro, p, q]
                if not last:
                    ghost_x[new, c, ro, q] = px[ro, q] - s * gx[ro, q]
            if not last:
                for p in range(2):
                    ghost_r[new, c, p, q] = res[4, p, q] - s * u[4, p, q]
                ghost_c[new, c, q] = px[4, q] - s * gx[4, q]

    def absorb(step, c):
        new = step % 2
        first, last = step == 0, step == n_steps
        for q in range(2):
            i = 2 * c + q
            row = slice(i, i + 1)

            def spot(ref_row, mask):
                return keep(mask, jnp.broadcast_to(ref_row, (8, half_y)))

            if not first:
                from_low = recv_r[step, 1, i]
                from_left = recv_x[step, 1, i]
                corner = spot(recv_c[step, 3, row], corner0)
                vec[new, c, 0, 0, q] += (
                    keep(~upper, from_low) + keep(first_x, from_left) + corner
                )
                vec[new, c, 0, 1, q] += keep(~upper, roll_s(from_low, 4))
                for ro in range(1, 4):
                    vec[new, c, ro, 0, q] += keep(first_x, roll_s(from_left, -ro))
            if not last:
                from_up = recv_r[step, 0, i]
                from_right = recv_x[step, 0, i]
                add0 = keep(upper, roll_s(from_up, 4))
                add1 = keep(upper, from_up)
                edge = keep(last_x, roll_s(from_right, 3))
                far = (
                    spot(recv_r[step, 0, 2 * comps, row], corner7)
                    + spot(recv_x[step, 0, 2 * comps, row], corner7)
                    + spot(recv_c[step, 0, row], corner7)
                )
                if not first:
                    add0 = (
                        add0
                        + spot(recv_x[step, 1, 2 * comps, row], corner4)
                        + spot(recv_c[step, 1, row], corner4)
                    )
                    edge = (
                        edge
                        + spot(recv_r[step, 1, 2 * comps, row], corner3)
                        + spot(recv_c[step, 2, row], corner3)
                    )
                    add0 = add0 + ghost_r[new, c, 0, q]
                    add1 = add1 + ghost_r[new, c, 1, q]
                    edge = edge + ghost_x[new, c, 0, q]
                    far = far + ghost_c[new, c, q]
                ghost_r[new, c, 0, q] = add0 * up_f
                ghost_r[new, c, 1, q] = add1 * up_f
                ghost_x[new, c, 0, q] = edge * right_f
                ghost_c[new, c, q] = far * both_f
                for ro in range(1, 4):
                    edge = keep(last_x, roll_s(from_right, 3 - ro))
                    if not first:
                        edge = edge + ghost_x[new, c, ro, q]
                    ghost_x[new, c, ro, q] = edge * right_f

    def to_native(k):
        cur = k % 2
        for c in range(comps):
            for ro in range(4):
                for p in range(2):
                    for q in range(2):
                        v = vec[cur, c, ro, p, q]
                        for h in range(2):
                            work[n_prev + k, q, native(c, ro, p, h), :] = v[4 * h : 4 * h + 4]

    def out_copy(k):
        return pltpu.make_async_copy(back.at[k - 1], out_ref.at[k - 1], out_sem.at[k - 1])

    def write_out(k):
        z = jnp.concatenate([work[n_prev + k, 0], work[n_prev + k, 1]], 1)
        back[k - 1] = exact_dot(z, join_perm)
        out_copy(k).start()

    lane16 = lax.broadcasted_iota(jnp.int32, (16, half_y), 1)
    row16 = lax.broadcasted_iota(jnp.int32, (16, half_y), 0)

    def gram_row(i):
        def chunk(t, acc):
            at = pl.ds(pl.multiple_of(8 * t, 8), 8)
            for q in range(2):
                mine = work[i, q, at, :]
                acc = tuple(
                    acc[j] + mine * (mine if j == i else work[j, q, at, :]) for j in range(i + 1)
                )
            return acc

        acc = lax.fori_loop(
            0, rows // 8, chunk, (jnp.zeros((8, half_y), F32),) * (i + 1), unroll=4
        )
        sums = [jnp.sum(a, axis=0, keepdims=True) for a in acc]
        sums.append(jnp.zeros((16 - len(sums), half_y), F32))
        total = jnp.sum(jnp.concatenate(sums, 0), axis=1, keepdims=True)
        hit = jnp.logical_or(lane16 == i * n_vec + row16, lane16 == row16 * n_vec + i)
        hit = jnp.logical_and(hit, row16 <= i)
        return jnp.sum(jnp.where(hit, jnp.broadcast_to(total, hit.shape), 0.0), 0, keepdims=True)

    res_copy.wait()
    split_columns(n_prev)
    for c in range(comps):
        for ro in range(4):
            for p in range(2):
                for q in range(2):
                    vec[0, c, ro, p, q] = jnp.concatenate(
                        [work[n_prev, q, native(c, ro, p, h), :] for h in range(2)], 0
                    )
    zero_row = jnp.zeros((8, half_y), F32)
    send_r[0, 0, 2 * comps] = zero_row
    send_x[0, 0, 2 * comps] = zero_row
    for c in range(comps):
        for q in range(2):
            i = 2 * c + q
            send_r[0, 0, i] = jnp.where(upper, roll_s(vec[0, c, 0, 1, q], 4), vec[0, c, 0, 0, q])
            send_x[0, 0, i] = pack_x([vec[0, c, ro, 0, q] for ro in range(4)], 0)
            send_c[0, 0, i : i + 1] = vec[0, c, 0, 0, q, 0:1]

    pl.semaphore_wait(barrier, n_dev - 1)
    start_round(0)
    prev_copy.wait()
    for i in range(n_prev):
        split_columns(i)
    finish_round(0)
    for c in range(comps):
        absorb(0, c)

    total = jnp.zeros((1, half_y), F32)
    for k in range(n_steps):
        for c in range(comps):
            apply(k, c)
        start_round(k + 1)
        if k == 0:
            for i in range(n_prev + 1):
                total = total + gram_row(i)
        else:
            to_native(k)
            write_out(k)
            total = total + gram_row(n_prev + k)
        finish_round(k + 1)
        for c in range(comps):
            absorb(k + 1, c)

    to_native(n_steps)
    total = total + gram_row(n_vec - 1)
    gram_send[...] = total

    def gram_copy(d):
        return pltpu.make_async_remote_copy(
            src_ref=gram_send,
            dst_ref=gram_recv.at[d - 1],
            send_sem=gram_sems.at[0],
            recv_sem=gram_sems.at[1],
            device_id=other(d),
            device_id_type=MESH,
        )

    def scatter(d, carry):
        gram_copy(d).start()
        return carry

    lax.fori_loop(1, n_dev, scatter, 0)
    write_out(n_steps)
    for step in range(n_steps + 1):
        for d in dirs_of(step):

            @pl.when(inside(*d))
            def _(d=d, step=step):
                copy_of(step, d).wait_send()

    for i in range(2):
        pltpu.make_async_copy(gram_recv, gram_recv, gram_sems.at[i]).wait()
    full = (total + jnp.sum(gram_recv[...], axis=0)) * (1.0 / (rows * 2 * half_y * n_dev))
    for i in range(n_vec):
        line = full if i == 0 else pltpu.roll(full, half_y - i * n_vec, 1)
        gram_ref[i : i + 1, :] = line[:, :n_vec]
    for k in range(1, n_steps + 1):
        out_copy(k).wait()


def on_device(residual, prev_basis, layer_ids, viscosity, shifts):
    n_lat = lax.axis_size("lat")
    n_rad = lax.axis_size("rad")
    comps, node_r, node_x, node_y = residual.shape
    n_prev = prev_basis.shape[0]
    n_steps = shifts.shape[0]
    n_vec = n_prev + n_steps + 1
    rows = comps * node_r * node_x
    half_y = node_y // 2
    assert node_r == 8 and node_x == 8 and half_y == 128
    rounds = n_steps + 1
    tile = (8, half_y)
    vmem = pltpu.VMEM
    any_spec = pl.BlockSpec(memory_space=pl.ANY)
    vmem_spec = pl.BlockSpec(memory_space=pltpu.VMEM)
    smem_spec = pl.BlockSpec(memory_space=pltpu.SMEM)
    out, gram = pl.pallas_call(
        functools.partial(kernel, n_lat, n_rad, n_steps, n_prev, comps),
        out_shape=(
            jax.ShapeDtypeStruct((n_steps, rows, node_y), F32),
            jax.ShapeDtypeStruct((n_vec, n_vec), F32),
        ),
        in_specs=[any_spec, any_spec, vmem_spec, smem_spec, smem_spec],
        out_specs=(any_spec, vmem_spec),
        scratch_shapes=[
            vmem((n_prev + 1, rows, node_y), F32),
            vmem((n_steps, rows, node_y), F32),
            vmem((n_vec, 2, rows, half_y), F32),
            vmem((2, comps, 4, 2, 2) + tile, F32),
            vmem((2, comps, 2, 2) + tile, F32),
            vmem((2, comps, 4, 2) + tile, F32),
            vmem((2, comps, 2) + tile, F32),
            vmem((2, 9) + tile, F32),
            vmem((rounds, 2, 2 * comps + 1) + tile, F32),
            vmem((rounds, 2, 2 * comps + 1) + tile, F32),
            vmem((rounds, 4) + tile, F32),
            vmem((rounds, 2, 2 * comps + 1) + tile, F32),
            vmem((rounds, 2, 2 * comps + 1) + tile, F32),
            vmem((rounds, 4) + tile, F32),
            vmem((1, half_y), F32),
            vmem((n_lat * n_rad - 1, 1, half_y), F32),
            pltpu.SemaphoreType.DMA((2,)),
            pltpu.SemaphoreType.DMA((n_steps,)),
            pltpu.SemaphoreType.DMA((rounds, 8)),
            pltpu.SemaphoreType.DMA((rounds, 8)),
            pltpu.SemaphoreType.DMA((2,)),
        ],
        compiler_params=pltpu.CompilerParams(
            collective_id=0, has_side_effects=True, vmem_limit_bytes=48 * 1024 * 1024
        ),
    )(
        residual.reshape(rows, node_y),
        prev_basis.reshape(n_prev, rows, node_y),
        layer_ids,
        viscosity,
        shifts,
    )
    return out.reshape((n_steps,) + residual.shape), gram


def solution(mesh):
    placed = (
        P(None, "rad", "lat", None),
        P(None, None, "rad", "lat", None),
        P("rad", "lat", None),
        P(),
        P(),
    )
    return jax.shard_map(
        on_device,
        mesh=mesh,
        in_specs=placed,
        out_specs=(P(None, None, "rad", "lat", None), P()),
        check_vma=False,
    )
```

profile of v0, /device:TPU:0, one launch (start us, length us, event | category | flops | bytes accessed | tf_op | source)
XLA Modules:
  0.0 36.5 jit_solution(5828884560586686441)
XLA Ops:
  0.6 0.0 copy-start.3
  0.6 0.0 copy-start.4
  0.7 0.6 %copy-done.3 = f32[8]{0:T(128)S(1)} copy-done((f32[8]{0:T(128)S(1)}, f32[8]{0:T(128)}, u32[]{:S(2)}) %copy-start.3) | copy-done | bytes 56
  1.3 0.0 copy-done.4
  1.3 0.0 copy-start
  1.3 1.1 %copy-done = f32[4,3,8,8,256]{4,3,2,1,0:T(8,128)S(1)} copy-done((f32[4,3,8,8,256]{4,3,2,1,0:T(8,128)S(1)}, f32[4,3,8,8,256]{4,3,2,1,0:T(8,128)}, u32[]{:S(2)}) %copy-start) | copy-done | bytes 786456
  2.4 0.0 copy-start.1
  2.4 0.9 %copy-done.1 = f32[3,8,8,256]{3,2,1,0:T(8,128)S(1)} copy-done((f32[3,8,8,256]{3,2,1,0:T(8,128)S(1)}, f32[3,8,8,256]{3,2,1,0:T(8,128)}, u32[]{:S(2)}) %copy-start.1) | copy-done | bytes 196632
  3.4 0.0 copy-start.2
  3.4 0.7 %copy-done.2 = s32[4,4,128]{2,1,0:T(4,128)S(1)} copy-done((s32[4,4,128]{2,1,0:T(4,128)S(1)}, s32[4,4,128]{2,1,0:T(4,128)}, u32[]{:S(2)}) %copy-start.2) | copy-done | bytes 8216
  4.1 30.9 %shard_map.68 = (f32[4,192,256]{2,1,0:T(8,128)S(1)}, f32[9,9]{1,0:T(8,128)S(1)}) custom-call(f32[192,256]{1,0:T(8,128)S(1)} %bitcast.5, f32[4,192,256]{2,1,0:T(8,128)S(1)} %bitcast.3, s32[4,4,128]{2,1,0:T(4,128)S(1)} %copy-done.2, f32[8]{0:T(128)S(1)} %copy-done.3, f32[4]{0:T(128)S(1)} %copy-done.4), custom_call_target="tpu_custom_call" | custom-call | tf_op jit(solution)/shard_map/pallas_call | solution.py:500
  35.0 0.9 %copy.9 = f32[4,3,8,8,256]{4,3,2,1,0:T(8,128)} copy(f32[4,3,8,8,256]{4,3,2,1,0:T(8,128)S(1)} %bitcast.4) | data formatting | bytes 1572864
  35.9 0.6 %copy.10 = f32[9,9]{1,0:T(8,128)} copy(f32[9,9]{1,0:T(8,128)S(1)} %get-tuple-element.9) | data formatting | bytes 648
Async XLA Ops:
  0.6 0.7 %copy-start.3 = (f32[8]{0:T(128)S(1)}, f32[8]{0:T(128)}, u32[]{:S(2)}) copy-start(f32[8]{0:T(128)} %visc_ref.1) | copy-start | bytes 100
  0.6 0.7 %copy-start.4 = (f32[4]{0:T(128)S(1)}, f32[4]{0:T(128)}, u32[]{:S(2)}) copy-start(f32[4]{0:T(128)} %shift_ref.1) | copy-start | bytes 52
  1.3 1.1 %copy-start = (f32[4,3,8,8,256]{4,3,2,1,0:T(8,128)S(1)}, f32[4,3,8,8,256]{4,3,2,1,0:T(8,128)}, u32[]{:S(2)}) copy-start(f32[4,3,8,8,256]{4,3,2,1,0:T(8,128)} %param.6) | copy-start | bytes 2359300
  2.4 0.9 %copy-start.1 = (f32[3,8,8,256]{3,2,1,0:T(8,128)S(1)}, f32[3,8,8,256]{3,2,1,0:T(8,128)}, u32[]{:S(2)}) copy-start(f32[3,8,8,256]{3,2,1,0:T(8,128)} %param.5) | copy-start | bytes 589828
  3.4 0.7 %copy-start.2 = (s32[4,4,128]{2,1,0:T(4,128)S(1)}, s32[4,4,128]{2,1,0:T(4,128)}, u32[]{:S(2)}) copy-start(s32[4,4,128]{2,1,0:T(4,128)} %ids_ref.1) | copy-start | bytes 24580
where the time goes:
time: 36.7 us; the launch traced here: 36.5 us
  Pallas kernels  30.9 us (84%)
  local copies, waits for them, and re-layouts  4.89 us (13%)
  between operations  0.66 us (2%)
    pallas_call x1, Pallas kernels, on_device(): pl.pallas_call(functools.partial(kernel, n_lat, n_rad, n_steps, n_prev, c...  30.9 us
    unnamed x12, local copies, waits for them, and re-layouts  4.89 us

commit v1 on v0

--- a/solution.py
+++ b/solution.py
@@ -48,13 +48,16 @@
     comps,
     res_ref,
     prev_ref,
-    ids_ref,
-    visc_ref,
-    shift_ref,
+    ids_hbm,
+    visc_hbm,
+    shift_hbm,
     out_ref,
     gram_ref,
     stage,
     back,
+    ids_ref,
+    visc_ref,
+    shift_ref,
     work,
     vec,
     ghost_r,
@@ -86,6 +89,14 @@
     res_copy = pltpu.make_async_copy(res_ref, stage.at[n_prev], in_sem.at[0])
     res_copy.start()
     prev_copy = pltpu.make_async_copy(prev_ref, stage.at[pl.ds(0, n_prev)], in_sem.at[1])
+    small_copies = [
+        pltpu.make_async_copy(a, b, in_sem.at[2 + i])
+        for i, (a, b) in enumerate(
+            ((ids_hbm, ids_ref), (visc_hbm, visc_ref), (shift_hbm, shift_ref))
+        )
+    ]
+    for copy in small_copies:
+        copy.start()
     prev_copy.start()
 
     recv_r[...] = jnp.zeros_like(recv_r)
@@ -153,26 +164,18 @@
                 key = tuple(sorted((a, b, c)))
                 if key != (0, 0, 0) and key not in kinds:
                     kinds[key] = len(kinds)
-    for e in range(2):
-        ids = jnp.concatenate([ids_ref[e], ids_ref[2 + e]], 0)
-        eta = jnp.zeros((8, half_y), F32)
-        for layer in range(visc_ref.shape[0]):
-            eta = eta + jnp.where(ids == layer, visc_ref[layer], 0.0)
-        for key, i in kinds.items():
-            scaled[e, i] = eta * weight(*key)
-
-    def copy_of(step, d):
+    def copy_of(step, c, d):
         if d in R_DIRS:
-            a, b = send_r.at[step, R_DIRS[d]], recv_r.at[step, R_DIRS[d]]
+            a, b = send_r.at[step, c, R_DIRS[d]], recv_r.at[step, c, R_DIRS[d]]
         elif d in X_DIRS:
-            a, b = send_x.at[step, X_DIRS[d]], recv_x.at[step, X_DIRS[d]]
+            a, b = send_x.at[step, c, X_DIRS[d]], recv_x.at[step, c, X_DIRS[d]]
         else:
-            a, b = send_c.at[step, C_DIRS[d]], recv_c.at[step, C_DIRS[d]]
+            a, b = send_c.at[step, c, C_DIRS[d]], recv_c.at[step, c, C_DIRS[d]]
         return pltpu.make_async_remote_copy(
             src_ref=a,
             dst_ref=b,
-            send_sem=send_sem.at[step, SLOT[d]],
-            recv_sem=recv_sem.at[step, SLOT[d]],
+            send_sem=send_sem.at[step, c, SLOT[d]],
+            recv_sem=recv_sem.at[step, c, SLOT[d]],
             device_id={"lat": lat + d[1], "rad": rad + d[0]},
             device_id_type=MESH,
         )
@@ -191,19 +194,19 @@
         wanted = FIRST if step == 0 else (LAST if step == n_steps else DIRS)
         return [d for d in order if d in wanted]
 
-    def start_round(step):
+    def start_round(step, c):
         for d in dirs_of(step):
 
             @pl.when(inside(*d))
             def _(d=d):
-                copy_of(step, d).start()
-
-    def finish_round(step):
+                copy_of(step, c, d).start()
+
+    def finish_round(step, c):
         for d in dirs_of(step):
 
             @pl.when(inside(-d[0], -d[1]))
             def _(d=d):
-                copy_of(step, d).wait_recv()
+                copy_of(step, c, d).wait_recv()
 
     def pack_x(vals, at):
         out = None
@@ -278,21 +281,22 @@
         step = k + 1
         last = step == n_steps
         for q in range(2):
-            i = 2 * c + q
-            row = slice(i, i + 1)
-            send_r[step, 1, i] = jnp.where(upper, res[4, 1, q], roll_s(res[4, 0, q], 4))
-            send_r[step, 1, 2 * comps, row] = px[4, q][7:8]
-            send_x[step, 1, i] = pack_x([px[ro, q] for ro in range(4)], 3)
-            send_x[step, 1, 2 * comps, row] = px[4, q][7:8]
-            send_c[step, 3, row] = px[4, q][7:8]
+            face = slice(8 * q, 8 * q + 8)
+            edge = slice(16 + q, 17 + q)
+            row = slice(q, q + 1)
+            send_r[step, c, 1, face] = jnp.where(upper, res[4, 1, q], roll_s(res[4, 0, q], 4))
+            send_r[step, c, 1, edge] = px[4, q][7:8]
+            send_x[step, c, 1, face] = pack_x([px[ro, q] for ro in range(4)], 3)
+            send_x[step, c, 1, edge] = px[4, q][7:8]
+            send_c[step, c, 3, row] = px[4, q][7:8]
             if not last:
-                send_r[step, 0, i] = jnp.where(upper, roll_s(res[0, 1, q], 4), res[0, 0, q])
-                send_r[step, 0, 2 * comps, row] = px[0, q][3:4]
-                send_x[step, 0, i] = pack_x([res[ro, 0, q] for ro in range(4)], 0)
-                send_x[step, 0, 2 * comps, row] = res[4, 0, q][4:5]
-                send_c[step, 0, row] = res[0, 0, q][0:1]
-                send_c[step, 1, row] = px[0, q][3:4]
-                send_c[step, 2, row] = res[4, 0, q][4:5]
+                send_r[step, c, 0, face] = jnp.where(upper, roll_s(res[0, 1, q], 4), res[0, 0, q])
+                send_r[step, c, 0, edge] = px[0, q][3:4]
+                send_x[step, c, 0, face] = pack_x([res[ro, 0, q] for ro in range(4)], 0)
+                send_x[step, c, 0, edge] = res[4, 0, q][4:5]
+                send_c[step, c, 0, row] = res[0, 0, q][0:1]
+                send_c[step, c, 1, row] = px[0, q][3:4]
+                send_c[step, c, 2, row] = res[4, 0, q][4:5]
             for ro in range(4):
                 for p in range(2):
                     vec[new, c, ro, p, q] = res[ro, p, q] - s * u[ro, p, q]
@@ -307,16 +311,17 @@
         new = step % 2
         first, last = step == 0, step == n_steps
         for q in range(2):
-            i = 2 * c + q
-            row = slice(i, i + 1)
+            face = slice(8 * q, 8 * q + 8)
+            line = slice(16 + q, 17 + q)
+            row = slice(q, q + 1)
 
             def spot(ref_row, mask):
                 return keep(mask, jnp.broadcast_to(ref_row, (8, half_y)))
 
             if not first:
-                from_low = recv_r[step, 1, i]
-                from_left = recv_x[step, 1, i]
-                corner = spot(recv_c[step, 3, row], corner0)
+                from_low = recv_r[step, c, 1, face]
+                from_left = recv_x[step, c, 1, face]
+                corner = spot(recv_c[step, c, 3, row], corner0)
                 vec[new, c, 0, 0, q] += (
                     keep(~upper, from_low) + keep(first_x, from_left) + corner
                 )
@@ -324,26 +329,26 @@
                 for ro in range(1, 4):
                     vec[new, c, ro, 0, q] += keep(first_x, roll_s(from_left, -ro))
             if not last:
-                from_up = recv_r[step, 0, i]
-                from_right = recv_x[step, 0, i]
+                from_up = recv_r[step, c, 0, face]
+                from_right = recv_x[step, c, 0, face]
                 add0 = keep(upper, roll_s(from_up, 4))
                 add1 = keep(upper, from_up)
                 edge = keep(last_x, roll_s(from_right, 3))
                 far = (
-                    spot(recv_r[step, 0, 2 * comps, row], corner7)
-                    + spot(recv_x[step, 0, 2 * comps, row], corner7)
-                    + spot(recv_c[step, 0, row], corner7)
+                    spot(recv_r[step, c, 0, line], corner7)
+                    + spot(recv_x[step, c, 0, line], corner7)
+                    + spot(recv_c[step, c, 0, row], corner7)
                 )
                 if not first:
                     add0 = (
                         add0
-                        + spot(recv_x[step, 1, 2 * comps, row], corner4)
-                        + spot(recv_c[step, 1, row], corner4)
+                        + spot(recv_x[step, c, 1, line], corner4)
+                        + spot(recv_c[step, c, 1, row], corner4)
                     )
                     edge = (
                         edge
-                        + spot(recv_r[step, 1, 2 * comps, row], corner3)
-                        + spot(recv_c[step, 2, row], corner3)
+                        + spot(recv_r[step, c, 1, line], corner3)
+                        + spot(recv_c[step, c, 2, row], corner3)
                     )
                     add0 = add0 + ghost_r[new, c, 0, q]
                     add1 = add1 + ghost_r[new, c, 1, q]
@@ -409,30 +414,41 @@
                     vec[0, c, ro, p, q] = jnp.concatenate(
                         [work[n_prev, q, native(c, ro, p, h), :] for h in range(2)], 0
                     )
-    zero_row = jnp.zeros((8, half_y), F32)
-    send_r[0, 0, 2 * comps] = zero_row
-    send_x[0, 0, 2 * comps] = zero_row
+    zero_rows = jnp.zeros((2, half_y), F32)
     for c in range(comps):
+        send_r[0, c, 0, 16:18] = zero_rows
+        send_x[0, c, 0, 16:18] = zero_rows
         for q in range(2):
-            i = 2 * c + q
-            send_r[0, 0, i] = jnp.where(upper, roll_s(vec[0, c, 0, 1, q], 4), vec[0, c, 0, 0, q])
-            send_x[0, 0, i] = pack_x([vec[0, c, ro, 0, q] for ro in range(4)], 0)
-            send_c[0, 0, i : i + 1] = vec[0, c, 0, 0, q, 0:1]
+            face = slice(8 * q, 8 * q + 8)
+            send_r[0, c, 0, face] = jnp.where(
+                upper, roll_s(vec[0, c, 0, 1, q], 4), vec[0, c, 0, 0, q]
+            )
+            send_x[0, c, 0, face] = pack_x([vec[0, c, ro, 0, q] for ro in range(4)], 0)
+            send_c[0, c, 0, q : q + 1] = vec[0, c, 0, 0, q, 0:1]
 
     pl.semaphore_wait(barrier, n_dev - 1)
-    start_round(0)
+    for c in range(comps):
+        start_round(0, c)
+    for copy in small_copies:
+        copy.wait()
+    for e in range(2):
+        ids = jnp.concatenate([ids_ref[e], ids_ref[2 + e]], 0)
+        eta = jnp.zeros((8, half_y), F32)
+        for layer in range(visc_ref.shape[0]):
+            eta = eta + jnp.where(ids == layer, visc_ref[layer], 0.0)
+        for key, i in kinds.items():
+            scaled[e, i] = eta * weight(*key)
     prev_copy.wait()
     for i in range(n_prev):
         split_columns(i)
-    finish_round(0)
-    for c in range(comps):
-        absorb(0, c)
 
     total = jnp.zeros((1, half_y), F32)
     for k in range(n_steps):
         for c in range(comps):
+            finish_round(k, c)
+            absorb(k, c)
             apply(k, c)
-        start_round(k + 1)
+            start_round(k + 1, c)
         if k == 0:
             for i in range(n_prev + 1):
                 total = total + gram_row(i)
@@ -440,9 +456,9 @@
             to_native(k)
             write_out(k)
             total = total + gram_row(n_prev + k)
-        finish_round(k + 1)
-        for c in range(comps):
-            absorb(k + 1, c)
+    for c in range(comps):
+        finish_round(n_steps, c)
+        absorb(n_steps, c)
 
     to_native(n_steps)
     total = total + gram_row(n_vec - 1)
@@ -465,11 +481,12 @@
     lax.fori_loop(1, n_dev, scatter, 0)
     write_out(n_steps)
     for step in range(n_steps + 1):
-        for d in dirs_of(step):
-
-            @pl.when(inside(*d))
-            def _(d=d, step=step):
-                copy_of(step, d).wait_send()
+        for c in range(comps):
+            for d in dirs_of(step):
+
+                @pl.when(inside(*d))
+                def _(c=c, d=d, step=step):
+                    copy_of(step, c, d).wait_send()
 
     for i in range(2):
         pltpu.make_async_copy(gram_recv, gram_recv, gram_sems.at[i]).wait()
@@ -494,42 +511,44 @@
     rounds = n_steps + 1
     tile = (8, half_y)
     vmem = pltpu.VMEM
-    any_spec = pl.BlockSpec(memory_space=pl.ANY)
+    hbm_spec = pl.BlockSpec(memory_space=pltpu.HBM)
     vmem_spec = pl.BlockSpec(memory_space=pltpu.VMEM)
-    smem_spec = pl.BlockSpec(memory_space=pltpu.SMEM)
     out, gram = pl.pallas_call(
         functools.partial(kernel, n_lat, n_rad, n_steps, n_prev, comps),
         out_shape=(
             jax.ShapeDtypeStruct((n_steps, rows, node_y), F32),
             jax.ShapeDtypeStruct((n_vec, n_vec), F32),
         ),
-        in_specs=[any_spec, any_spec, vmem_spec, smem_spec, smem_spec],
-        out_specs=(any_spec, vmem_spec),
+        in_specs=[hbm_spec] * 5,
+        out_specs=(hbm_spec, vmem_spec),
         scratch_shapes=[
             vmem((n_prev + 1, rows, node_y), F32),
             vmem((n_steps, rows, node_y), F32),
+            vmem(layer_ids.shape, jnp.int32),
+            pltpu.SMEM(viscosity.shape, F32),
+            pltpu.SMEM(shifts.shape, F32),
             vmem((n_vec, 2, rows, half_y), F32),
             vmem((2, comps, 4, 2, 2) + tile, F32),
             vmem((2, comps, 2, 2) + tile, F32),
             vmem((2, comps, 4, 2) + tile, F32),
             vmem((2, comps, 2) + tile, F32),
             vmem((2, 9) + tile, F32),
-            vmem((rounds, 2, 2 * comps + 1) + tile, F32),
-            vmem((rounds, 2, 2 * comps + 1) + tile, F32),
-            vmem((rounds, 4) + tile, F32),
-            vmem((rounds, 2, 2 * comps + 1) + tile, F32),
-            vmem((rounds, 2, 2 * comps + 1) + tile, F32),
-            vmem((rounds, 4) + tile, F32),
+            vmem((rounds, comps, 2, 18, half_y), F32),
+            vmem((rounds, comps, 2, 18, half_y), F32),
+            vmem((rounds, comps, 4, 2, half_y), F32),
+            vmem((rounds, comps, 2, 18, half_y), F32),
+            vmem((rounds, comps, 2, 18, half_y), F32),
+            vmem((rounds, comps, 4, 2, half_y), F32),
             vmem((1, half_y), F32),
             vmem((n_lat * n_rad - 1, 1, half_y), F32),
-            pltpu.SemaphoreType.DMA((2,)),
+            pltpu.SemaphoreType.DMA((5,)),
             pltpu.SemaphoreType.DMA((n_steps,)),
-            pltpu.SemaphoreType.DMA((rounds, 8)),
-            pltpu.SemaphoreType.DMA((rounds, 8)),
+            pltpu.SemaphoreType.DMA((rounds, comps, 8)),
+            pltpu.SemaphoreType.DMA((rounds, comps, 8)),
             pltpu.SemaphoreType.DMA((2,)),
         ],
         compiler_params=pltpu.CompilerParams(
-            collective_id=0, has_side_effects=True, vmem_limit_bytes=48 * 1024 * 1024
+            collective_id=0, has_side_effects=True, vmem_limit_bytes=67043328
         ),
     )(
         residual.reshape(rows, node_y),

time: 36.7 us -> 33.9 us (0.924)
  local copies, waits for them, and re-layouts: 4.89 us -> 2.67 us
  Pallas kernels: 30.9 us -> 30.5 us
    unnamed x12 -> x4, local copies, waits for them, and re-layouts: 4.89 us -> 2.67 us
    pallas_call x1, Pallas kernels: 30.9 us -> 30.5 us  [on_device(): pl.pallas_call(functools.partial(kernel, n_lat, n_rad, n_steps, n_prev, c...]
where the time goes in v1:
time: 33.9 us; the launch traced here: 33.8 us
  Pallas kernels  30.5 us (90%)
  local copies, waits for them, and re-layouts  2.67 us (8%)
  between operations  0.65 us (2%)
    pallas_call x1, Pallas kernels, on_device(): pl.pallas_call(functools.partial(kernel, n_lat, n_rad, n_steps, n_prev, c...  30.5 us
    unnamed x4, local copies, waits for them, and re-layouts  2.67 us

profile of v1, /device:TPU:0, one launch (start us, length us, event | category | flops | bytes accessed | tf_op | source)
XLA Modules:
  0.0 33.8 jit_solution(7916998671151354719)
XLA Ops:
  0.6 30.5 %shard_map.68 = (f32[4,192,256]{2,1,0:T(8,128)}, f32[9,9]{1,0:T(8,128)}) custom-call(f32[192,256]{1,0:T(8,128)} %bitcast.5, f32[4,192,256]{2,1,0:T(8,128)} %bitcast.3, s32[4,4,128]{2,1,0:T(4,128)} %ids_hbm.1, f32[8]{0:T(128)} %visc_hbm.1, f32[4]{0:T(128)} %shift_hbm.1), custom_call_target="tpu_custom_call" | custom-call | tf_op jit(solution)/shard_map/pallas_call | solution.py:516
  31.1 0.0 copy-start
  31.1 2.1 %copy.9 = f32[4,3,8,8,256]{4,3,2,1,0:T(8,128)} copy(f32[4,3,8,8,256]{4,3,2,1,0:T(8,128)} %bitcast.4) | data formatting | bytes 1572864
  33.2 0.0 copy-done
  33.2 0.6 %copy.10 = f32[9,9]{1,0:T(8,128)} copy(f32[9,9]{1,0:T(8,128)S(1)} %copy-done) | data formatting | bytes 648
Async XLA Ops:
  31.1 2.1 %copy-start = (f32[9,9]{1,0:T(8,128)S(1)}, f32[9,9]{1,0:T(8,128)}, u32[]{:S(2)}) copy-start(f32[9,9]{1,0:T(8,128)} %get-tuple-element.9) | copy-start | bytes 976

commit v2 on v1

--- a/solution.py
+++ b/solution.py
@@ -54,7 +54,6 @@
     out_ref,
     gram_ref,
     stage,
-    back,
     ids_ref,
     visc_ref,
     shift_ref,
@@ -73,7 +72,6 @@
     gram_send,
     gram_recv,
     in_sem,
-    out_sem,
     send_sem,
     recv_sem,
     gram_sems,
@@ -105,15 +103,23 @@
 
     barrier = pltpu.get_barrier_semaphore()
 
-    def other(d):
-        t = lax.rem(me + d, n_dev)
-        return {"lat": t // n_rad, "rad": lax.rem(t, n_rad)}
-
-    def greet(d, carry):
-        pl.semaphore_signal(barrier, inc=1, device_id=other(d), device_id_type=MESH)
-        return carry
-
-    lax.fori_loop(1, n_dev, greet, 0)
+    rad_targets = [lax.rem(rad + d, n_rad) for d in range(n_rad)]
+
+    def each_other(visit):
+        def row(ahead, carry):
+            lat_target = lax.rem(lat + ahead, n_lat)
+            for d in range(n_rad):
+                visit(ahead * n_rad + d - 1, {"lat": lat_target, "rad": rad_targets[d]})
+            return carry
+
+        lax.fori_loop(1, n_lat, row, 0, unroll=n_lat <= 8)
+        for d in range(1, n_rad):
+            visit(d - 1, {"lat": lat, "rad": rad_targets[d]})
+
+    def greet(slot, device):
+        pl.semaphore_signal(barrier, inc=1, device_id=device, device_id_type=MESH)
+
+    each_other(greet)
 
     sub = lax.broadcasted_iota(jnp.int32, (8, half_y), 0)
     lane = lax.broadcasted_iota(jnp.int32, (8, half_y), 1)
@@ -374,13 +380,9 @@
                         for h in range(2):
                             work[n_prev + k, q, native(c, ro, p, h), :] = v[4 * h : 4 * h + 4]
 
-    def out_copy(k):
-        return pltpu.make_async_copy(back.at[k - 1], out_ref.at[k - 1], out_sem.at[k - 1])
-
     def write_out(k):
         z = jnp.concatenate([work[n_prev + k, 0], work[n_prev + k, 1]], 1)
-        back[k - 1] = exact_dot(z, join_perm)
-        out_copy(k).start()
+        out_ref[k - 1] = exact_dot(z, join_perm)
 
     lane16 = lax.broadcasted_iota(jnp.int32, (16, half_y), 1)
     row16 = lax.broadcasted_iota(jnp.int32, (16, half_y), 0)
@@ -464,21 +466,17 @@
     total = total + gram_row(n_vec - 1)
     gram_send[...] = total
 
-    def gram_copy(d):
-        return pltpu.make_async_remote_copy(
+    def scatter(slot, device):
+        pltpu.make_async_remote_copy(
             src_ref=gram_send,
-            dst_ref=gram_recv.at[d - 1],
+            dst_ref=gram_recv.at[slot],
             send_sem=gram_sems.at[0],
             recv_sem=gram_sems.at[1],
-            device_id=other(d),
+            device_id=device,
             device_id_type=MESH,
-        )
-
-    def scatter(d, carry):
-        gram_copy(d).start()
-        return carry
-
-    lax.fori_loop(1, n_dev, scatter, 0)
+        ).start()
+
+    each_other(scatter)
     write_out(n_steps)
     for step in range(n_steps + 1):
         for c in range(comps):
@@ -494,8 +492,6 @@
     for i in range(n_vec):
         line = full if i == 0 else pltpu.roll(full, half_y - i * n_vec, 1)
         gram_ref[i : i + 1, :] = line[:, :n_vec]
-    for k in range(1, n_steps + 1):
-        out_copy(k).wait()
 
 
 def on_device(residual, prev_basis, layer_ids, viscosity, shifts):
@@ -516,14 +512,13 @@
     out, gram = pl.pallas_call(
         functools.partial(kernel, n_lat, n_rad, n_steps, n_prev, comps),
         out_shape=(
-            jax.ShapeDtypeStruct((n_steps, rows, node_y), F32),
-            jax.ShapeDtypeStruct((n_vec, n_vec), F32),
+            pltpu.VMEM((n_steps, rows, node_y), F32),
+            pltpu.VMEM((n_vec, n_vec), F32),
         ),
         in_specs=[hbm_spec] * 5,
-        out_specs=(hbm_spec, vmem_spec),
+        out_specs=(vmem_spec, vmem_spec),
         scratch_shapes=[
             vmem((n_prev + 1, rows, node_y), F32),
-            vmem((n_steps, rows, node_y), F32),
             vmem(layer_ids.shape, jnp.int32),
             pltpu.SMEM(viscosity.shape, F32),
             pltpu.SMEM(shifts.shape, F32),
@@ -542,13 +537,12 @@
             vmem((1, half_y), F32),
             vmem((n_lat * n_rad - 1, 1, half_y), F32),
             pltpu.SemaphoreType.DMA((5,)),
-            pltpu.SemaphoreType.DMA((n_steps,)),
             pltpu.SemaphoreType.DMA((rounds, comps, 8)),
             pltpu.SemaphoreType.DMA((rounds, comps, 8)),
             pltpu.SemaphoreType.DMA((2,)),
         ],
         compiler_params=pltpu.CompilerParams(
-            collective_id=0, has_side_effects=True, vmem_limit_bytes=67043328
+            collective_id=0, has_side_effects=True, vmem_limit_bytes=65000000
         ),
     )(
         residual.reshape(rows, node_y),

time: 33.9 us -> 31.5 us (0.929)
  Pallas kernels: 30.5 us -> 29.2 us
  local copies, waits for them, and re-layouts: 2.67 us -> 1.48 us
    pallas_call x1, Pallas kernels: 30.5 us -> 29.2 us  [on_device(): pl.pallas_call(functools.partial(kernel, n_lat, n_rad, n_steps, n_prev, c...]
    unnamed x4 -> x2, local copies, waits for them, and re-layouts: 2.67 us -> 1.48 us
where the time goes in v2:
time: 31.5 us; the launch traced here: 31.3 us
  Pallas kernels  29.2 us (93%)
  local copies, waits for them, and re-layouts  1.48 us (5%)
  between operations  0.64 us (2%)
    pallas_call x1, Pallas kernels, on_device(): pl.pallas_call(functools.partial(kernel, n_lat, n_rad, n_steps, n_prev, c...  29.2 us
    unnamed x2, local copies, waits for them, and re-layouts  1.48 us

profile of v2, /device:TPU:0, one launch (start us, length us, event | category | flops | bytes accessed | tf_op | source)
XLA Modules:
  0.0 31.3 jit_solution(6864086514270209640)
XLA Ops:
  0.6 29.2 %shard_map.68 = (f32[4,192,256]{2,1,0:T(8,128)S(1)}, f32[9,9]{1,0:T(8,128)S(1)}) custom-call(f32[192,256]{1,0:T(8,128)} %bitcast.5, f32[4,192,256]{2,1,0:T(8,128)} %bitcast.4, s32[4,4,128]{2,1,0:T(4,128)} %ids_hbm.1, f32[8]{0:T(128)} %visc_hbm.1, f32[4]{0:T(128)} %shift_hbm.1), custom_call_target="tpu_custom_call" | custom-call | tf_op jit(solution)/shard_map/pallas_call | solution.py:512
  29.9 0.9 %copy.9 = f32[4,3,8,8,256]{4,3,2,1,0:T(8,128)} copy(f32[4,3,8,8,256]{4,3,2,1,0:T(8,128)S(1)} %bitcast.3) | data formatting | bytes 1572864
  30.7 0.6 %copy.10 = f32[9,9]{1,0:T(8,128)} copy(f32[9,9]{1,0:T(8,128)S(1)} %get-tuple-element.7) | data formatting | bytes 648
